TPU v7x, 32 devices: a whole 2x2x4 slice. The times are simulated.
32 devices in a mesh: ev: 2 (over core), own: 16 (over z, y, x).
Axes of the slice: x: 2, y: 2, z: 4, core: 2. Of those that a mesh axis runs over, the one named last changes fastest.
Arguments:
- ground_up: bfloat16 [8192, 4096], P('own', 'ev'), parts along dimension 1, may hold values from 0.049804688 to 2
- item_site: int32 [8192], P('own'), may hold values from 0 to 127
- item_profile: int32 [8192], P('own'), may hold values from 0 to 127
- site_owner: int32 [2048, 1], P('own'), may hold values from 0 to 15; in each aligned block of 128 rows (0 to 127, 128 to 255, ...) at most 16 rows name the same one
- site_slot: int32 [2048], P('own'), may hold values from 0 to 63
- site_profile: int32 [2048], P('own'), may hold values from 0 to 127
- policy_owner: int32 [1024, 1], P('own'), may hold values from 0 to 15; in each aligned block of 64 rows (0 to 63, 64 to 127, ...) at most 12 rows name the same one
- policy_slot: int32 [1024], P('own'), may hold values from 0 to 1
- policy_profile: int32 [1024], P('own'), may hold values from 0 to 127
- program_profile: int32 [32], P('own'), may hold values from 0 to 127
- term_table: float32 [4, 3, 128], replicated, may hold values from 0 to 90, as said below
Outputs:
- policy_loss: bfloat16 [1024, 4096], P('own', 'ev'), parts along dimension 1
- program_loss: float32 [32, 4096], P('own', 'ev'), parts along dimension 1
There are 2 independent parts, one for each index of `ev`. A program takes and returns all parts, laid end to end along the dimension named above; an argument that names none is the same for every part. Nothing has to cross between parts.
Inputs may be any that keep to these rules, and one draw needn't show every extreme that they name: `site_owner`: among the 128 sites of one owner, no owner of policies appears more than 16 times; some owner appears exactly 16 times in some owner's sites. `policy_owner`: among the 64 policies of one owner, no owner of programs appears more than 12 times; some owner appears exactly 12 times in some owner's policies. `term_table`: deductibles are 0 or more, limits positive, shares between 0.5 and 1.
All inputs are finite; a program needn't handle non-finite values.
Results may differ from a plain program's by a relative error of at most 0.0051.
Values may be sent and summed in bfloat16 or wider, within the bound.
A program may use at most 64 MiB of HBM per device.

v0:
```python
import jax
import jax.numpy as jnp
from jax import lax
from jax.sharding import PartitionSpec as P


def apply_terms(gross_loss, terms_table, tier_index, profile):
    profile_iota = jnp.arange(terms_table.shape[2], dtype=jnp.int32)
    picker = profile[:, None] == profile_iota[None, :]
    deduct = jnp.sum(jnp.where(picker, terms_table[tier_index, 0][None, :], 0.0), axis=1)[:, None]
    ceiling = jnp.sum(jnp.where(picker, terms_table[tier_index, 1][None, :], 0.0), axis=1)[:, None]
    portion = jnp.sum(jnp.where(picker, terms_table[tier_index, 2][None, :], 0.0), axis=1)[:, None]
    return portion * jnp.minimum(jnp.maximum(gross_loss - deduct, 0.0), ceiling)


def pack_rows(values, target_dev, inner_slot, owners, capacity):
    member = (target_dev[:, None] == jnp.arange(owners, dtype=jnp.int32)[None, :]).astype(jnp.int32)
    before = jnp.cumsum(member, axis=0) - member
    position = jnp.sum(before * member, axis=1)
    target = target_dev * capacity + position
    placer = jnp.arange(owners * capacity, dtype=jnp.int32)[:, None] == target[None, :]
    packed = jnp.dot(
        placer.astype(jnp.bfloat16), values, preferred_element_type=jnp.float32
    ).astype(jnp.bfloat16)
    labels = jnp.sum(jnp.where(placer, (inner_slot + 1)[None, :], 0), axis=1) - 1
    return (
        packed.reshape(owners, capacity, values.shape[1]),
        labels.astype(jnp.bfloat16).reshape(owners, capacity),
    )


def sum_rows(received, labels, slot_count):
    flattened = received.reshape(-1, received.shape[2])
    slot_marks = labels.reshape(-1).astype(jnp.int32)
    picker = (jnp.arange(slot_count, dtype=jnp.int32)[:, None] == slot_marks[None, :]).astype(
        jnp.bfloat16
    )
    return jnp.dot(picker, flattened, preferred_element_type=jnp.float32)


def shards(
    ground_up,
    item_site,
    item_profile,
    site_owner,
    site_slot,
    site_profile,
    policy_owner,
    policy_slot,
    policy_profile,
    program_profile,
    term_table,
):
    owners = lax.axis_size("own")
    covered = apply_terms(ground_up.astype(jnp.float32), term_table, 0, item_profile).astype(
        jnp.bfloat16
    )
    site_total = site_profile.shape[0]
    grouping = (jnp.arange(site_total, dtype=jnp.int32)[:, None] == item_site[None, :]).astype(
        jnp.bfloat16
    )
    site_gross = jnp.dot(grouping, covered, preferred_element_type=jnp.float32)
    site_net = apply_terms(site_gross, term_table, 1, site_profile).astype(jnp.bfloat16)
    capacity = 2 * site_total // owners
    packed, labels = pack_rows(site_net, site_owner[:, 0], site_slot, owners, capacity)
    arrived, arrived_labels = (
        lax.all_to_all(packed, "own", split_axis=0, concat_axis=0, tiled=True),
        lax.all_to_all(labels, "own", split_axis=0, concat_axis=0, tiled=True),
    )
    policy_total = policy_profile.shape[0]
    policy_gross = sum_rows(arrived, arrived_labels, policy_total)
    policy_loss = apply_terms(policy_gross, term_table, 2, policy_profile).astype(jnp.bfloat16)
    program_total = program_profile.shape[0]
    program_capacity = 3 * policy_total // owners
    sent_rows, sent_labels = pack_rows(
        policy_loss, policy_owner[:, 0], policy_slot, owners, program_capacity
    )
    got_rows, got_labels = (
        lax.all_to_all(sent_rows, "own", split_axis=0, concat_axis=0, tiled=True),
        lax.all_to_all(sent_labels, "own", split_axis=0, concat_axis=0, tiled=True),
    )
    program_gross = sum_rows(got_rows, got_labels, program_total)
    program_loss = apply_terms(program_gross, term_table, 3, program_profile)
    return (policy_loss, program_loss)


def solution(mesh):
    placed = (
        P("own", "ev"),
        P("own"),
        P("own"),
        P("own", None),
        P("own"),
        P("own"),
        P("own", None),
        P("own"),
        P("own"),
        P("own"),
        P(),
    )
    return jax.shard_map(
        shards,
        mesh=mesh,
        in_specs=placed,
        out_specs=(P("own", "ev"), P("own", "ev")),
        check_vma=False,
    )
```

profile of v0, /device:TPU:0, one launch (start us, length us, event | category | flops | bytes accessed | tf_op | source)
XLA Modules:
  0.0 90.2 jit_solution(8755179414698308574)
XLA Ops:
  0.6 0.7 fusion.18
  1.5 0.8 select_reduce_fusion.8
  2.4 0.7 multiply_add_fusion.1
  3.2 0.7 convert_element_type.95
  3.9 8.3 %all-to-all-start = ((bf16[16,1,16]{2,1,0:T(2,128)(2,1)}), bf16[16,1,16]{2,1,0:T(2,128)(2,1)S(1)}, u32[]{:S(2)}, u32[]{:S(2)}) async-start(bf16[16,1,16]{2,1,0:T(2,128)(2,1)} %convert_element_type.95), calls=%async_computation | async-start | bytes 16384 | tf_op jit(solution)/shard_map/all_to_all | solution.py:68
  12.2 0.9 slice_bitcast_fusion.1
  13.1 0.9 select_reduce_fusion.7
  14.0 1.1 %select_reduce_fusion.2 = (f32[512]{0:T(512)S(1)}, f32[512]{0:T(512)S(1)}, f32[512]{0:T(512)S(1)}) fusion(f32[128]{0:T(128)S(1)} %get-tuple-element.22, s32[512]{0:T(512)} %param.13, f32[128]{0:T(128)S(1)} %get-tuple-element.20, f32[128]{0:T(128)S(1)} %get-tuple-element.21), kind=kLoop, calls=%fused_computation.23 | loop fusion | flops 457216 | bytes 9728 | tf_op jit(solution)/shard_map/reduce_sum | solution.py:12
  15.0 4.0 %convolution_convert_fusion = bf16[256,2048]{1,0:T(8,128)(2,1)} fusion(bf16[512,2048]{1,0:T(8,128)(2,1)} %param.11, f32[512]{0:T(512)S(1)} %get-tuple-element.3, f32[512]{0:T(512)S(1)} %get-tuple-element.4, f32[512]{0:T(512)S(1)} %get-tuple-element.2, f32[128]{0:T(128)S(1)} %get-tuple-element.12, f32[128]{0:T(128)S(1)} %get-tuple-element.13, ...), kind=kOutput, calls=%fused_computation.1 | convolution fusion | flops 410877952 | bytes 3155968 | tf_op jit(solution)/shard_map/dot_general | solution.py:22
  19.1 0.4 all-to-all-done
  19.5 6.7 %all-to-all-start.1 = ((bf16[16,16,2048]{2,1,0:T(8,128)(2,1)}), bf16[16,16,2048]{2,1,0:T(8,128)(2,1)S(1)}, u32[]{:S(2)}, u32[]{:S(2)}) async-start(bf16[16,16,2048]{2,1,0:T(8,128)(2,1)} %bitcast.8), calls=%async_computation.1 | async-start | bytes 2097152 | tf_op jit(solution)/shard_map/all_to_all | solution.py:67
  26.3 0.2 select_reduce_fusion.9
  26.6 0.7 convert_element_type.96
  27.4 0.2 select_reduce_fusion.12
  27.7 22.2 %all-to-all-done.1 = bf16[16,16,2048]{2,1,0:T(8,128)(2,1)S(1)} async-done(((bf16[16,16,2048]{2,1,0:T(8,128)(2,1)}), bf16[16,16,2048]{2,1,0:T(8,128)(2,1)S(1)}, u32[]{:S(2)}, u32[]{:S(2)}) %all-to-all-start.1) | async-done | bytes 1048608 | tf_op jit(solution)/shard_map/all_to_all | solution.py:67
  49.9 5.9 %all-to-all-start.2 = ((bf16[16,1,12]{2,1,0:T(2,128)(2,1)}), bf16[16,1,12]{2,1,0:T(2,128)(2,1)S(1)}, u32[]{:S(2)}, u32[]{:S(2)}) async-start(bf16[16,1,12]{2,1,0:T(2,128)(2,1)} %convert_element_type.96), calls=%async_computation.2 | async-start | bytes 16384 | tf_op jit(solution)/shard_map/all_to_all | solution.py:80
  55.9 0.3 fusion.7
  56.2 0.5 convolution_convert_fusion.1
  56.7 1.2 %reshape.123 = bf16[16,12,2048]{2,1,0:T(8,128)(2,1)} reshape(bf16[192,2048]{1,0:T(8,128)(2,1)S(1)} %convolution_convert_fusion.1) | data formatting | bytes 1572864 | tf_op jit(solution)/shard_map/reshape | solution.py:27
  57.8 5.2 %all-to-all-done.2 = bf16[16,1,12]{2,1,0:T(2,128)(2,1)S(1)} async-done(((bf16[16,1,12]{2,1,0:T(2,128)(2,1)}), bf16[16,1,12]{2,1,0:T(2,128)(2,1)S(1)}, u32[]{:S(2)}, u32[]{:S(2)}) %all-to-all-start.2) | async-done | bytes 416 | tf_op jit(solution)/shard_map/all_to_all | solution.py:80
  63.1 3.7 %all-to-all-start.3 = ((bf16[16,12,2048]{2,1,0:T(8,128)(2,1)}), bf16[16,12,2048]{2,1,0:T(8,128)(2,1)S(1)}, u32[]{:S(2)}, u32[]{:S(2)}) async-start(bf16[16,12,2048]{2,1,0:T(8,128)(2,1)} %reshape.123), calls=%async_computation.3 | async-start | bytes 2097152 | tf_op jit(solution)/shard_map/all_to_all | solution.py:79
  66.8 0.2 select_reduce_fusion.15
  67.1 22.1 %all-to-all-done.3 = bf16[16,12,2048]{2,1,0:T(8,128)(2,1)S(1)} async-done(((bf16[16,12,2048]{2,1,0:T(8,128)(2,1)}), bf16[16,12,2048]{2,1,0:T(8,128)(2,1)S(1)}, u32[]{:S(2)}, u32[]{:S(2)}) %all-to-all-start.3) | async-done | bytes 786464 | tf_op jit(solution)/shard_map/all_to_all | solution.py:79
  89.4 0.8 fusion.10
  (24 shorter events, 1.0 us)
Async XLA Ops:
  3.9 15.6 %all-to-all-start = ((bf16[16,1,16]{2,1,0:T(2,128)(2,1)}), bf16[16,1,16]{2,1,0:T(2,128)(2,1)S(1)}, u32[]{:S(2)}, u32[]{:S(2)}) async-start(bf16[16,1,16]{2,1,0:T(2,128)(2,1)} %convert_element_type.95), calls=%async_computation | async-start | bytes 16384 | tf_op jit(solution)/shard_map/all_to_all | solution.py:68
  19.1 7.1 %copy-start.1 = (s32[64,1]{0,1:T(1,128)S(1)}, s32[64,1]{0,1:T(1,128)}, u32[]{:S(2)}) copy-start(s32[64,1]{0,1:T(1,128)} %param.17) | copy-start | bytes 772
  19.1 7.4 %copy-start.4 = (s32[64]{0:T(128)S(1)}, s32[64]{0:T(128)}, u32[]{:S(2)}) copy-start(s32[64]{0:T(128)} %param.18) | copy-start | bytes 772
  19.1 8.3 %copy-start.2 = (s32[64]{0:T(128)S(1)}, s32[64]{0:T(128)}, u32[]{:S(2)}) copy-start(s32[64]{0:T(128)} %param.19) | copy-start | bytes 772
  19.5 30.5 %all-to-all-start.1 = ((bf16[16,16,2048]{2,1,0:T(8,128)(2,1)}), bf16[16,16,2048]{2,1,0:T(8,128)(2,1)S(1)}, u32[]{:S(2)}, u32[]{:S(2)}) async-start(bf16[16,16,2048]{2,1,0:T(8,128)(2,1)} %bitcast.8), calls=%async_computation.1 | async-start | bytes 2097152 | tf_op jit(solution)/shard_map/all_to_all | solution.py:67
  49.9 13.1 %all-to-all-start.2 = ((bf16[16,1,12]{2,1,0:T(2,128)(2,1)}), bf16[16,1,12]{2,1,0:T(2,128)(2,1)S(1)}, u32[]{:S(2)}, u32[]{:S(2)}) async-start(bf16[16,1,12]{2,1,0:T(2,128)(2,1)} %convert_element_type.96), calls=%async_computation.2 | async-start | bytes 16384 | tf_op jit(solution)/shard_map/all_to_all | solution.py:80
  56.2 6.9 %copy-start = (bf16[64,2048]{1,0:T(8,128)(2,1)}, bf16[64,2048]{1,0:T(8,128)(2,1)S(1)}, u32[]{:S(2)}) copy-start(bf16[64,2048]{1,0:T(8,128)(2,1)S(1)} %fusion.7) | copy-start | bytes 786436
  56.7 10.1 %copy-start.3 = (s32[2]{0:T(128)S(1)}, s32[2]{0:T(128)}, u32[]{:S(2)}) copy-start(s32[2]{0:T(128)} %param.20) | copy-start | bytes 28
  63.1 26.1 %all-to-all-start.3 = ((bf16[16,12,2048]{2,1,0:T(8,128)(2,1)}), bf16[16,12,2048]{2,1,0:T(8,128)(2,1)S(1)}, u32[]{:S(2)}, u32[]{:S(2)}) async-start(bf16[16,12,2048]{2,1,0:T(8,128)(2,1)} %reshape.123), calls=%async_computation.3 | async-start | bytes 2097152 | tf_op jit(solution)/shard_map/all_to_all | solution.py:79
where the time goes:
time: 90.7 us; the launch traced here: 90.2 us
  waiting for transfers between devices  50 us (55%)
  starting transfers between devices  24.6 us (27%)
  matrix products  5.63 us (6%)
  other arithmetic  5.41 us (6%)
  local copies, waits for them, and re-layouts  3.8 us (4%)
    all_to_all x1, waiting for transfers between devices, shards(): lax.all_to_all(packed, 'own', split_axis=0, concat_axis=0, tiled=True)  22.2 us
    all_to_all x1, waiting for transfers between devices, shards(): lax.all_to_all(sent_rows, 'own', split_axis=0, concat_axis=0, tiled=True)  22.1 us
    all_to_all x1, starting transfers between devices, shards(): lax.all_to_all(labels, 'own', split_axis=0, concat_axis=0, tiled=True)  8.34 us
    all_to_all x1, starting transfers between devices, shards(): lax.all_to_all(packed, 'own', split_axis=0, concat_axis=0, tiled=True)  6.68 us
    all_to_all x1, starting transfers between devices, shards(): lax.all_to_all(sent_labels, 'own', split_axis=0, concat_axis=0, tiled=True)  5.91 us
    all_to_all x1, waiting for transfers between devices, shards(): lax.all_to_all(sent_labels, 'own', split_axis=0, concat_axis=0, tiled=True)  5.25 us
    dot_general x2, matrix products, pack_rows(): jnp.dot(placer.astype(jnp.bfloat16), values, preferred_element_type=jnp.f...  4.5 us
    all_to_all x1, starting transfers between devices, shards(): lax.all_to_all(sent_rows, 'own', split_axis=0, concat_axis=0, tiled=True)  3.65 us
  transfers between devices with their start and end apart: 4, of which 4 were waited for; matrix products, arithmetic and copies ran while one was open for 12% of the time, Pallas kernels for 0%

commit v1 on v0

--- a/solution.py
+++ b/solution.py
@@ -1,7 +1,345 @@
+import functools
+
 import jax
 import jax.numpy as jnp
 from jax import lax
+from jax.experimental import pallas as pl
+from jax.experimental.pallas import tpu as pltpu
 from jax.sharding import PartitionSpec as P
+
+LANES = 128
+META = 8
+f32 = jnp.float32
+bf16 = jnp.bfloat16
+
+
+def terms(x, deduct, ceiling, portion):
+    return portion * jnp.minimum(jnp.maximum(x - deduct, 0.0), ceiling)
+
+
+def kernel(
+    n,
+    pol,
+    prog,
+    ground,
+    ints,
+    table,
+    policy_out,
+    program_out,
+    chunks,
+    square,
+    item_terms,
+    site_terms,
+    policy_terms,
+    program_terms,
+    grouping,
+    meta,
+    send,
+    recv,
+    acc,
+    losses,
+    program_send,
+    load_sem,
+    meta_ss,
+    meta_rs,
+    site_ss,
+    site_rs,
+    pol_ss,
+    pol_rs,
+    prog_ss,
+    prog_rs,
+):
+    me = lax.axis_index("own")
+    groups = n // 2
+    mine = me // 2
+    half = groups // 2
+    items = ground.shape[0]
+    blocks = items // LANES
+    sites = send.shape[1]
+    width = send.shape[2]
+    wide = 2 * width
+
+    barrier = pltpu.get_barrier_semaphore()
+
+    def greet(k, c):
+        pl.semaphore_signal(barrier, inc=1, device_id={"own": lax.rem(me + k, n)})
+        return c
+
+    lax.fori_loop(1, n, greet, 0)
+
+    def load(i):
+        g = lax.rem(mine + half + i, groups)
+        return pltpu.make_async_copy(
+            ground.at[:, pl.ds(pl.multiple_of(g * wide, wide), wide)],
+            chunks.at[i],
+            load_sem.at[i],
+        )
+
+    def start_load(i, c):
+        load(i).start()
+        return c
+
+    lax.fori_loop(0, groups, start_load, 0)
+
+    square[...] = jnp.zeros_like(square)
+    for level in range(4):
+        square[3 * level : 3 * level + 3, :] = table[level]
+    columns = square[...].T
+    rows_iota = lax.broadcasted_iota(jnp.int32, (LANES, LANES), 0)
+
+    def look(profile_row, level):
+        pick = rows_iota == profile_row
+        return [
+            jnp.sum(
+                jnp.where(pick, columns[:, 3 * level + t : 3 * level + t + 1], 0.0),
+                axis=0,
+                keepdims=True,
+            )
+            for t in range(3)
+        ]
+
+    base = 2 * blocks
+    own_meta = [ints[base : base + 1, :].astype(f32)]
+    own_meta += look(ints[base + 2 : base + 3, :], 2)
+    own_meta += [ints[base + 3 : base + 4, :].astype(f32)]
+    own_meta += look(ints[base + 4 : base + 5, :], 3)
+    meta[me] = jnp.concatenate(own_meta, axis=0)
+
+    for b in range(blocks):
+        grouping[:, b * LANES : (b + 1) * LANES] = (rows_iota == ints[b : b + 1, :]).astype(bf16)
+        for t, row in enumerate(look(ints[blocks + b : blocks + b + 1, :], 0)):
+            square[3 * b + t : 3 * b + t + 1, :] = row
+    for t, row in enumerate(look(ints[base + 1 : base + 2, :], 1)):
+        square[3 * blocks + t : 3 * blocks + t + 1, :] = row
+    flipped = square[...].T
+    for t in range(3):
+        for b in range(blocks):
+            item_terms[t, b * LANES : (b + 1) * LANES, :] = jnp.broadcast_to(
+                flipped[:, 3 * b + t : 3 * b + t + 1], (LANES, LANES)
+            )
+        site_terms[t] = jnp.broadcast_to(
+            flipped[:, 3 * blocks + t : 3 * blocks + t + 1], (LANES, LANES)
+        )
+
+    pl.semaphore_wait(barrier, n - 1)
+
+    def meta_copy(d, s):
+        return pltpu.make_async_remote_copy(
+            meta.at[s], meta.at[s], meta_ss.at[d], meta_rs.at[s], device_id={"own": d}
+        )
+
+    def site_copy(d, s):
+        return pltpu.make_async_remote_copy(
+            send.at[d], recv.at[s], site_ss.at[d], site_rs.at[s], device_id={"own": d}
+        )
+
+    def policy_copy(d, s):
+        return pltpu.make_async_remote_copy(
+            losses.at[pl.ds(pl.multiple_of(d * pol, pol), pol), :],
+            policy_out.at[:, pl.ds(pl.multiple_of(s * width, width), width)],
+            pol_ss.at[d],
+            pol_rs.at[s],
+            device_id={"own": d},
+        )
+
+    def program_copy(d, s):
+        return pltpu.make_async_remote_copy(
+            program_send.at[d],
+            program_out.at[:, pl.ds(pl.multiple_of(s * width, width), width)],
+            prog_ss.at[d],
+            prog_rs.at[s],
+            device_id={"own": d},
+        )
+
+    def others(fn):
+        def step(k, c):
+            fn(lax.rem(me + k, n))
+            return c
+
+        lax.fori_loop(1, n, step, 0)
+
+    others(lambda d: meta_copy(d, me).start())
+
+    def sites_step(i, c):
+        load(i).wait()
+        g = lax.rem(mine + half + i, groups)
+        spread = [jnp.concatenate([item_terms[t]] * (wide // LANES), axis=1) for t in range(3)]
+        covered = terms(chunks[i].astype(f32), *spread).astype(bf16)
+        gross = jnp.dot(grouping[...], covered, preferred_element_type=f32)
+        site_spread = [jnp.concatenate([site_terms[t]] * (wide // LANES), axis=1) for t in range(3)]
+        net = terms(gross, *site_spread).astype(bf16)
+        for j in range(2):
+            d = 2 * g + j
+            piece = net[:, j * width : (j + 1) * width]
+
+            @pl.when(d == me)
+            def _():
+                recv[me] = piece
+
+            @pl.when(d != me)
+            def _():
+                send[d] = piece
+                site_copy(d, me).start()
+
+        return c
+
+    lax.fori_loop(0, groups, sites_step, 0)
+
+    others(lambda s: meta_copy(me, s).wait_recv())
+
+    meta_flat = meta[...].reshape(n * META, LANES)
+    turned = meta_flat.T
+    for o in range(n):
+        for t in range(3):
+            lane = o * META + 1 + t
+            policy_terms[t, o * pol : (o + 1) * pol, :] = jnp.broadcast_to(
+                turned[0:pol, lane : lane + 1], (pol, LANES)
+            )
+            lane = o * META + 5 + t
+            program_terms[o, t] = jnp.broadcast_to(turned[0:prog, lane : lane + 1], (prog, LANES))
+
+    policy_iota = lax.broadcasted_iota(jnp.int32, (n * pol, sites), 0).astype(f32)
+    order = [0]
+    for k in range(1, half + 1):
+        order += [k] if k == groups - k else [k, groups - k]
+    acc[...] = jnp.zeros_like(acc)
+
+    for k in order:
+        g = lax.rem(mine + k, groups)
+        for j in range(2):
+            s = 2 * g + j
+
+            @pl.when(s != me)
+            def _():
+                site_copy(me, s).wait_recv()
+
+        pick = jnp.concatenate(
+            [(policy_iota == meta[2 * g + j][0:1, :]).astype(bf16) for j in range(2)], axis=1
+        )
+        values = recv[pl.ds(2 * g, 2)].reshape(2 * sites, width)
+        acc[...] += jnp.dot(pick, values, preferred_element_type=f32)
+
+    def policy_step(i, c):
+        d = lax.rem(me + n // 2 + i, n)
+        at = pl.ds(pl.multiple_of(d * pol, pol), pol)
+        spread = [
+            jnp.concatenate([policy_terms[t, at, :]] * (width // LANES), axis=1) for t in range(3)
+        ]
+        losses[at, :] = terms(acc[at, :], *spread).astype(bf16)
+
+        @pl.when(d != me)
+        def _():
+            policy_copy(d, me).start()
+
+        return c
+
+    lax.fori_loop(0, n, policy_step, 0)
+    own_policy = pltpu.make_async_copy(
+        losses.at[pl.ds(pl.multiple_of(me * pol, pol), pol), :],
+        policy_out.at[:, pl.ds(pl.multiple_of(me * width, width), width)],
+        pol_rs.at[me],
+    )
+    own_policy.start()
+
+    program_iota = lax.broadcasted_iota(jnp.int32, (n * prog, pol), 0).astype(f32)
+    marks = [
+        (program_iota == meta_flat[o * META + 4 : o * META + 5, 0:pol]).astype(bf16)
+        for o in range(n)
+    ]
+    program_gross = jnp.dot(jnp.concatenate(marks, axis=1), losses[...], preferred_element_type=f32)
+    for o in range(n):
+        spread = [
+            jnp.concatenate([program_terms[o, t]] * (width // LANES), axis=1) for t in range(3)
+        ]
+        program_send[o] = terms(program_gross[o * prog : (o + 1) * prog, :], *spread)
+    others(lambda d: program_copy(d, me).start())
+    own_program = pltpu.make_async_copy(
+        program_send.at[me],
+        program_out.at[:, pl.ds(pl.multiple_of(me * width, width), width)],
+        prog_rs.at[me],
+    )
+    own_program.start()
+
+    def finish(d):
+        meta_copy(d, me).wait_send()
+        site_copy(d, me).wait_send()
+        policy_copy(d, me).wait_send()
+        program_copy(d, me).wait_send()
+        policy_copy(me, d).wait_recv()
+        program_copy(me, d).wait_recv()
+
+    others(finish)
+    own_policy.wait()
+    own_program.wait()
+
+
+def exchange(
+    ground_up,
+    item_site,
+    item_profile,
+    site_owner,
+    site_slot,
+    site_profile,
+    policy_owner,
+    policy_slot,
+    policy_profile,
+    program_profile,
+    term_table,
+):
+    n = lax.axis_size("own")
+    items, cols = ground_up.shape
+    sites = site_profile.shape[0]
+    pol = policy_profile.shape[0]
+    prog = program_profile.shape[0]
+    width = cols // n
+    blocks = items // LANES
+
+    def row(v):
+        return jnp.pad(v, (0, LANES - v.shape[0])).reshape(1, LANES)
+
+    ints = jnp.concatenate(
+        [
+            item_site.reshape(blocks, LANES),
+            item_profile.reshape(blocks, LANES),
+            row(site_owner[:, 0] * pol + site_slot),
+            row(site_profile),
+            row(policy_profile),
+            row(policy_owner[:, 0] * prog + policy_slot),
+            row(program_profile),
+        ],
+        axis=0,
+    )
+    vmem = pl.BlockSpec(memory_space=pltpu.VMEM)
+    anyspec = pl.BlockSpec(memory_space=pl.ANY)
+    dma = pltpu.SemaphoreType.DMA
+    return pl.pallas_call(
+        functools.partial(kernel, n, pol, prog),
+        out_shape=(
+            jax.ShapeDtypeStruct((pol, cols), bf16),
+            jax.ShapeDtypeStruct((prog, cols), f32),
+        ),
+        in_specs=[anyspec, vmem, vmem],
+        out_specs=(anyspec, anyspec),
+        scratch_shapes=[
+            pltpu.VMEM((n // 2, items, 2 * width), bf16),
+            pltpu.VMEM((LANES, LANES), f32),
+            pltpu.VMEM((3, items, LANES), f32),
+            pltpu.VMEM((3, sites, LANES), f32),
+            pltpu.VMEM((3, n * pol, LANES), f32),
+            pltpu.VMEM((n, 3, prog, LANES), f32),
+            pltpu.VMEM((sites, items), bf16),
+            pltpu.VMEM((n, META, LANES), f32),
+            pltpu.VMEM((n, sites, width), bf16),
+            pltpu.VMEM((n, sites, width), bf16),
+            pltpu.VMEM((n * pol, width), f32),
+            pltpu.VMEM((n * pol, width), bf16),
+            pltpu.VMEM((n, prog, width), f32),
+            dma((n // 2,)),
+        ]
+        + [dma((n,))] * 8,
+        compiler_params=pltpu.CompilerParams(collective_id=0, has_side_effects=True),
+        name="loss_terms",
+    )(ground_up, ints, term_table)
 
 
 def apply_terms(gross_loss, terms_table, tier_index, profile):
@@ -98,8 +436,19 @@
         P("own"),
         P(),
     )
+
+    def body(ground_up, item_site, item_profile, *rest):
+        n = lax.axis_size("own")
+        items, cols = ground_up.shape
+        sites, pol = rest[2].shape[0], rest[5].shape[0]
+        prog = rest[6].shape[0]
+        fits = cols % (n * LANES) == 0 and items % LANES == 0 and sites == LANES
+        fits = fits and pol <= LANES and pol % 16 == 0 and prog <= 8
+        fits = fits and n % 4 == 0 and n * META <= LANES and 3 * items <= LANES * (LANES - 3)
+        return (exchange if fits else shards)(ground_up, item_site, item_profile, *rest)
+
     return jax.shard_map(
-        shards,
+        body,
         mesh=mesh,
         in_specs=placed,
         out_specs=(P("own", "ev"), P("own", "ev")),

time: 90.7 us -> 41.9 us (0.46)
  waiting for transfers between devices: 50 us -> 0 us
  Pallas kernels: 0 us -> 31.9 us
  starting transfers between devices: 24.6 us -> 0 us
  matrix products: 5.63 us -> 0 us
  other arithmetic: 5.41 us -> 1.37 us
  local copies, waits for them, and re-layouts: 3.8 us -> 7.5 us
    all_to_all x4 -> x0, waiting for transfers between devices: 50 us -> none  [the longest x1 22.2 us: shards(): lax.all_to_all(packed, 'own', split_axis=0, concat_axis=0, tiled=True)]
    pallas_call x0 -> x1, Pallas kernels: none -> 31.9 us  [exchange(): pl.pallas_call(functools.partial(kernel, n, pol, prog), out_shape=(jax.Sh...]
    all_to_all x4 -> x0, starting transfers between devices: 24.6 us -> none  [the longest x1 8.34 us: shards(): lax.all_to_all(labels, 'own', split_axis=0, concat_axis=0, tiled=True)]
    dot_general x4 -> x0, matrix products: 5.63 us -> none  [the longest x2 4.5 us: pack_rows(): jnp.dot(placer.astype(jnp.bfloat16), values, preferred_element_type=jnp.f...]
    unnamed x10 -> x3, local copies, waits for them, and re-layouts: 0.02 us -> 4.28 us
    reduce_sum x8 -> x0, other arithmetic: 3.55 us -> none  [the longest x4 2.34 us: apply_terms(): jnp.sum(jnp.where(picker, terms_table[tier_index, 2][None, :], 0.0), axis=1)]
    concatenate x0 -> x1, local copies, waits for them, and re-layouts: none -> 2.55 us  [exchange(): jnp.concatenate([item_site.reshape(blocks, LANES), item_profile.reshape(b...]
    convert_element_type x4 -> x0, local copies, waits for them, and re-layouts: 1.56 us -> none  [the longest x2 1.39 us: pack_rows(): labels.astype(jnp.bfloat16).reshape(owners, capacity)]
  transfers between devices with their start and end apart: 4 -> 0, of which waited for: 4 -> 0; matrix products, arithmetic and copies ran while one was open for 12% -> 0% of each run, Pallas kernels for 0% -> 0%
where the time goes in v1:
time: 41.9 us; the launch traced here: 41.4 us
  Pallas kernels  31.9 us (76%)
  local copies, waits for them, and re-layouts  7.5 us (18%)
  other arithmetic  1.37 us (3%)
  between operations  0.64 us (2%)
    pallas_call x1, Pallas kernels, exchange(): pl.pallas_call(functools.partial(kernel, n, pol, prog), out_shape=(jax.Sh...  31.9 us
    unnamed x3, local copies, waits for them, and re-layouts  4.28 us
    concatenate x1, local copies, waits for them, and re-layouts, exchange(): jnp.concatenate([item_site.reshape(blocks, LANES), item_profile.reshape(b...  2.55 us

profile of v1, /device:TPU:0, one launch (start us, length us, event | category | flops | bytes accessed | tf_op | source)
XLA Modules:
  0.0 41.4 jit_solution(17764009793611399298)
XLA Ops:
  0.6 0.7 %bitcast_add_fusion = s32[64]{0:T(128)S(1)} fusion(s32[64]{0:T(128)} %param.18, s32[64,1]{0,1:T(1,128)} %param.17), kind=kLoop, calls=%fused_computation | loop fusion | flops 128 | bytes 768 | tf_op jit(solution)/shard_map/add | solution.py:307
  1.3 0.7 %pad_bitcast_fusion.1 = (s32[1,128]{1,0:T(1,128)S(1)}, s32[1,128]{1,0:T(1,128)S(1)}) fusion(s32[64]{0:T(128)S(1)} %bitcast_add_fusion, s32[64]{0:T(128)} %param.19), kind=kLoop, calls=%fused_computation.4 | loop fusion | bytes 1536 | tf_op jit(solution)/shard_map/reshape | solution.py:298
  2.0 0.7 %fusion = (s32[1,128]{1,0:T(1,128)S(1)}, s32[1,128]{1,0:T(1,128)S(1)}) fusion(s32[128]{0:T(128)} %param.15, s32[128,1]{0,1:T(1,128)} %param.14, s32[2]{0:T(128)} %param.20), kind=kLoop, calls=%fused_computation.2 | loop fusion | flops 256 | bytes 2056 | tf_op jit(solution)/shard_map/reshape | solution.py:298
  2.7 2.6 %concatenate.3.ints = s32[13,128]{1,0:T(8,128)} concatenate(s32[4,128]{1,0:T(4,128)} %bitcast.17, s32[4,128]{1,0:T(4,128)} %bitcast.18, s32[1,128]{1,0:T(1,128)S(1)} %get-tuple-element.2, s32[1,128]{1,0:T(1,128)} %bitcast.19, s32[1,128]{1,0:T(1,128)S(1)} %get-tuple-element.5, s32[1,128]{1,0:T(1,128)S(1)} %get-tuple-element.4, s32[1,128]{1,0:T(1,128)S(1)} %get-tuple-element.3), dimensions={0} | concatenate | bytes 13312 | tf_op jit(solution)/shard_map/concatenate | solution.py:300
  5.2 1.3 %copy.13.table = f32[4,3,128]{2,1,0:T(4,128)} copy(f32[4,3,128]{2,0,1:T(4,128)} %param.21) | data formatting | bytes 12288 | tf_op args[10]
  6.5 31.9 %loss_terms.1 = (bf16[64,2048]{1,0:T(8,128)(2,1)}, f32[2,2048]{1,0:T(2,128)}) custom-call(bf16[512,2048]{1,0:T(8,128)(2,1)} %ground.1, s32[13,128]{1,0:T(8,128)} %concatenate.3.ints, f32[4,3,128]{2,1,0:T(4,128)} %copy.13.table), custom_call_target="tpu_custom_call" | custom-call | tf_op jit(solution)/shard_map/loss_terms/pallas_call | solution.py:315
  38.4 1.7 %copy.16 = bf16[64,2048]{1,0:T(8,128)(2,1)} copy(bf16[64,2048]{1,0:T(8,128)(2,1)} %get-tuple-element.8) | data formatting | bytes 524288
  40.1 1.3 %copy.17 = f32[2,2048]{1,0:T(2,128)} copy(f32[2,2048]{1,0:T(2,128)} %get-tuple-element.9) | data formatting | bytes 32768

commit v2 on v1

--- a/solution.py
+++ b/solution.py
@@ -9,6 +9,7 @@
 
 LANES = 128
 META = 8
+SMALL = 10
 f32 = jnp.float32
 bf16 = jnp.bfloat16
 
@@ -22,33 +23,37 @@
     pol,
     prog,
     ground,
-    ints,
-    table,
-    policy_out,
-    program_out,
-    chunks,
-    square,
-    item_terms,
-    site_terms,
-    policy_terms,
-    program_terms,
-    grouping,
-    meta,
-    send,
-    recv,
-    acc,
-    losses,
-    program_send,
-    load_sem,
-    meta_ss,
-    meta_rs,
-    site_ss,
-    site_rs,
-    pol_ss,
-    pol_rs,
-    prog_ss,
-    prog_rs,
+    *refs,
 ):
+    small_in, refs = refs[:SMALL], refs[SMALL:]
+    policy_out, program_out = refs[:2]
+    small, refs = refs[2 : 2 + SMALL], refs[2 + SMALL :]
+    (
+        chunks,
+        ids,
+        square,
+        item_terms,
+        site_terms,
+        policy_terms,
+        program_terms,
+        grouping,
+        meta,
+        send,
+        recv,
+        acc,
+        losses,
+        program_send,
+        small_sem,
+        load_sem,
+        meta_ss,
+        meta_rs,
+        site_ss,
+        site_rs,
+        pol_ss,
+        pol_rs,
+        prog_ss,
+        prog_rs,
+    ) = refs
     me = lax.axis_index("own")
     groups = n // 2
     mine = me // 2
@@ -67,6 +72,12 @@
 
     lax.fori_loop(1, n, greet, 0)
 
+    def fetch(i):
+        return pltpu.make_async_copy(small_in[i], small[i], small_sem.at[i])
+
+    for i in range(SMALL):
+        fetch(i).start()
+
     def load(i):
         g = lax.rem(mine + half + i, groups)
         return pltpu.make_async_copy(
@@ -80,10 +91,24 @@
         return c
 
     lax.fori_loop(0, groups, start_load, 0)
+    (
+        item_site,
+        item_profile,
+        site_owner,
+        site_slot,
+        site_profile,
+        policy_owner,
+        policy_slot,
+        policy_profile,
+        program_profile,
+        table,
+    ) = small
+    for i in range(SMALL):
+        fetch(i).wait()
 
     square[...] = jnp.zeros_like(square)
-    for level in range(4):
-        square[3 * level : 3 * level + 3, :] = table[level]
+    for t in range(3):
+        square[4 * t : 4 * t + 4, :] = table[t]
     columns = square[...].T
     rows_iota = lax.broadcasted_iota(jnp.int32, (LANES, LANES), 0)
 
@@ -91,25 +116,28 @@
         pick = rows_iota == profile_row
         return [
             jnp.sum(
-                jnp.where(pick, columns[:, 3 * level + t : 3 * level + t + 1], 0.0),
+                jnp.where(pick, columns[:, 4 * t + level : 4 * t + level + 1], 0.0),
                 axis=0,
                 keepdims=True,
             )
             for t in range(3)
         ]
 
-    base = 2 * blocks
-    own_meta = [ints[base : base + 1, :].astype(f32)]
-    own_meta += look(ints[base + 2 : base + 3, :], 2)
-    own_meta += [ints[base + 3 : base + 4, :].astype(f32)]
-    own_meta += look(ints[base + 4 : base + 5, :], 3)
+    ids[...] = jnp.zeros_like(ids)
+    ids[0:1, 0:pol] = policy_profile[...]
+    ids[1:2, 0:pol] = policy_owner[...] * prog + policy_slot[...]
+    ids[2:3, 0:prog] = program_profile[...]
+    own_meta = [(site_owner[...] * pol + site_slot[...]).astype(f32)]
+    own_meta += look(ids[0:1, :], 2)
+    own_meta += [ids[1:2, :].astype(f32)]
+    own_meta += look(ids[2:3, :], 3)
     meta[me] = jnp.concatenate(own_meta, axis=0)
 
     for b in range(blocks):
-        grouping[:, b * LANES : (b + 1) * LANES] = (rows_iota == ints[b : b + 1, :]).astype(bf16)
-        for t, row in enumerate(look(ints[blocks + b : blocks + b + 1, :], 0)):
+        grouping[:, b * LANES : (b + 1) * LANES] = (rows_iota == item_site[b : b + 1, :]).astype(bf16)
+        for t, row in enumerate(look(item_profile[b : b + 1, :], 0)):
             square[3 * b + t : 3 * b + t + 1, :] = row
-    for t, row in enumerate(look(ints[base + 1 : base + 2, :], 1)):
+    for t, row in enumerate(look(site_profile[...], 1)):
         square[3 * blocks + t : 3 * blocks + t + 1, :] = row
     flipped = square[...].T
     for t in range(3):
@@ -292,36 +320,39 @@
     pol = policy_profile.shape[0]
     prog = program_profile.shape[0]
     width = cols // n
-    blocks = items // LANES
 
     def row(v):
-        return jnp.pad(v, (0, LANES - v.shape[0])).reshape(1, LANES)
-
-    ints = jnp.concatenate(
-        [
-            item_site.reshape(blocks, LANES),
-            item_profile.reshape(blocks, LANES),
-            row(site_owner[:, 0] * pol + site_slot),
-            row(site_profile),
-            row(policy_profile),
-            row(policy_owner[:, 0] * prog + policy_slot),
-            row(program_profile),
-        ],
-        axis=0,
-    )
-    vmem = pl.BlockSpec(memory_space=pltpu.VMEM)
+        return v.reshape(-1, min(v.size, LANES))
+
+    inputs = [
+        row(v)
+        for v in (
+            item_site,
+            item_profile,
+            site_owner,
+            site_slot,
+            site_profile,
+            policy_owner,
+            policy_slot,
+            policy_profile,
+            program_profile,
+        )
+    ] + [term_table.transpose(1, 0, 2)]
+    vmemspec = pl.BlockSpec(memory_space=pltpu.VMEM)
     anyspec = pl.BlockSpec(memory_space=pl.ANY)
     dma = pltpu.SemaphoreType.DMA
     return pl.pallas_call(
         functools.partial(kernel, n, pol, prog),
         out_shape=(
-            jax.ShapeDtypeStruct((pol, cols), bf16),
-            jax.ShapeDtypeStruct((prog, cols), f32),
+            pltpu.VMEM((pol, cols), bf16),
+            pltpu.VMEM((prog, cols), f32),
         ),
-        in_specs=[anyspec, vmem, vmem],
-        out_specs=(anyspec, anyspec),
-        scratch_shapes=[
+        in_specs=[anyspec] * (1 + SMALL),
+        out_specs=(vmemspec, vmemspec),
+        scratch_shapes=[pltpu.VMEM(v.shape, v.dtype) for v in inputs]
+        + [
             pltpu.VMEM((n // 2, items, 2 * width), bf16),
+            pltpu.VMEM((8, LANES), jnp.int32),
             pltpu.VMEM((LANES, LANES), f32),
             pltpu.VMEM((3, items, LANES), f32),
             pltpu.VMEM((3, sites, LANES), f32),
@@ -334,12 +365,13 @@
             pltpu.VMEM((n * pol, width), f32),
             pltpu.VMEM((n * pol, width), bf16),
             pltpu.VMEM((n, prog, width), f32),
+            dma((SMALL,)),
             dma((n // 2,)),
         ]
         + [dma((n,))] * 8,
         compiler_params=pltpu.CompilerParams(collective_id=0, has_side_effects=True),
         name="loss_terms",
-    )(ground_up, ints, term_table)
+    )(ground_up, *inputs)
 
 
 def apply_terms(gross_loss, terms_table, tier_index, profile):

time: 41.9 us -> 33.3 us (0.79)
  local copies, waits for them, and re-layouts: 7.5 us -> 1.31 us
  other arithmetic: 1.37 us -> 0 us
  Pallas kernels: 31.9 us -> 31.2 us
    unnamed x3 -> x2, local copies, waits for them, and re-layouts: 4.28 us -> 1.31 us
    concatenate x1 -> x0, local copies, waits for them, and re-layouts: 2.55 us -> none  [exchange(): jnp.concatenate([item_site.reshape(blocks, LANES), item_profile.reshape(b...]
    pallas_call x1, Pallas kernels: 31.9 us -> 31.2 us  [exchange(): pl.pallas_call(functools.partial(kernel, n, pol, prog), out_shape=(pltpu....]
    reshape x1 -> x0, other arithmetic: 0.69 us -> none  [row(): return jnp.pad(v, (0, LANES - v.shape[0])).reshape(1, LANES)]
    add x1 -> x0, other arithmetic: 0.68 us -> none  [exchange(): policy_owner[:, 0] * prog + policy_slot]
    reshape x1 -> x0, local copies, waits for them, and re-layouts: 0.66 us -> none  [row(): return jnp.pad(v, (0, LANES - v.shape[0])).reshape(1, LANES)]
where the time goes in v2:
time: 33.3 us; the launch traced here: 33.1 us
  Pallas kernels  31.2 us (94%)
  local copies, waits for them, and re-layouts  1.31 us (4%)
  between operations  0.64 us (2%)
    pallas_call x1, Pallas kernels, exchange(): pl.pallas_call(functools.partial(kernel, n, pol, prog), out_shape=(pltpu....  31.2 us
    unnamed x2, local copies, waits for them, and re-layouts  1.31 us

profile of v2, /device:TPU:0, one launch (start us, length us, event | category | flops | bytes accessed | tf_op | source)
XLA Modules:
  0.0 33.1 jit_solution(4992501923506394192)
XLA Ops:
  0.6 31.2 %loss_terms.1 = (bf16[64,2048]{1,0:T(8,128)(2,1)S(1)}, f32[2,2048]{1,0:T(2,128)S(1)}) custom-call(bf16[512,2048]{1,0:T(8,128)(2,1)} %ground.1, s32[4,128]{1,0:T(4,128)} %bitcast.11, s32[4,128]{1,0:T(4,128)} %bitcast.12, s32[1,128]{1,0:T(1,128)} %bitcast.13, s32[1,128]{1,0:T(1,128)} %bitcast.14, s32[1,128]{1,0:T(1,128)} %bitcast.15, s32[1,64]{1,0:T(1,128)} %bitcast.16, ...), custom_call_target="tpu_custom_call" | custom-call | tf_op jit(solution)/shard_map/loss_terms/pallas_call | solution.py:344
  31.8 0.7 %copy.15 = bf16[64,2048]{1,0:T(8,128)(2,1)} copy(bf16[64,2048]{1,0:T(8,128)(2,1)S(1)} %get-tuple-element.2) | data formatting | bytes 524288
  32.5 0.6 %copy.16 = f32[2,2048]{1,0:T(2,128)} copy(f32[2,2048]{1,0:T(2,128)S(1)} %get-tuple-element.3) | data formatting | bytes 32768

commit v3 on v2

--- a/solution.py
+++ b/solution.py
@@ -8,7 +8,6 @@
 from jax.sharding import PartitionSpec as P
 
 LANES = 128
-META = 8
 SMALL = 10
 f32 = jnp.float32
 bf16 = jnp.bfloat16
@@ -16,6 +15,18 @@
 
 def terms(x, deduct, ceiling, portion):
     return portion * jnp.minimum(jnp.maximum(x - deduct, 0.0), ceiling)
+
+
+def across(me, k, n):
+    d, bit = 0, 1
+    while bit < n:
+        d = d + bit * lax.rem(lax.div(me, bit) + (k // bit) % 2, 2)
+        bit *= 2
+    return d
+
+
+def route(n):
+    return [k for i in range(n // 2) for k in (n // 2 + i, i) if k]
 
 
 def kernel(
@@ -125,13 +136,9 @@
 
     ids[...] = jnp.zeros_like(ids)
     ids[0:1, 0:pol] = policy_profile[...]
-    ids[1:2, 0:pol] = policy_owner[...] * prog + policy_slot[...]
-    ids[2:3, 0:prog] = program_profile[...]
-    own_meta = [(site_owner[...] * pol + site_slot[...]).astype(f32)]
-    own_meta += look(ids[0:1, :], 2)
-    own_meta += [ids[1:2, :].astype(f32)]
-    own_meta += look(ids[2:3, :], 3)
-    meta[me] = jnp.concatenate(own_meta, axis=0)
+    ids[0:1, pol : 2 * pol] = policy_owner[...] * prog + policy_slot[...]
+    ids[1:2, 0:prog] = program_profile[...]
+    meta[me] = jnp.concatenate([site_owner[...] * pol + site_slot[...], ids[0:1, :]], axis=0)
 
     for b in range(blocks):
         grouping[:, b * LANES : (b + 1) * LANES] = (rows_iota == item_site[b : b + 1, :]).astype(bf16)
@@ -139,17 +146,20 @@
             square[3 * b + t : 3 * b + t + 1, :] = row
     for t, row in enumerate(look(site_profile[...], 1)):
         square[3 * blocks + t : 3 * blocks + t + 1, :] = row
+    for t, row in enumerate(look(ids[1:2, :], 3)):
+        square[3 * blocks + 3 + t : 3 * blocks + 4 + t, :] = row
     flipped = square[...].T
     for t in range(3):
         for b in range(blocks):
             item_terms[t, b * LANES : (b + 1) * LANES, :] = jnp.broadcast_to(
                 flipped[:, 3 * b + t : 3 * b + t + 1], (LANES, LANES)
             )
+        program_terms[t] = jnp.broadcast_to(
+            flipped[0:prog, 3 * blocks + 3 + t : 3 * blocks + 4 + t], (prog, LANES)
+        )
         site_terms[t] = jnp.broadcast_to(
             flipped[:, 3 * blocks + t : 3 * blocks + t + 1], (LANES, LANES)
         )
-
-    pl.semaphore_wait(barrier, n - 1)
 
     def meta_copy(d, s):
         return pltpu.make_async_remote_copy(
@@ -185,8 +195,6 @@
             return c
 
         lax.fori_loop(1, n, step, 0)
-
-    others(lambda d: meta_copy(d, me).start())
 
     def sites_step(i, c):
         load(i).wait()
@@ -207,26 +215,33 @@
             @pl.when(d != me)
             def _():
                 send[d] = piece
-                site_copy(d, me).start()
 
         return c
 
     lax.fori_loop(0, groups, sites_step, 0)
 
+    pl.semaphore_wait(barrier, n - 1)
+
+    others(lambda d: meta_copy(d, me).start())
+
+    for k in route(n):
+        d = across(me, k, n)
+        site_copy(d, me).start()
+
     others(lambda s: meta_copy(me, s).wait_recv())
 
-    meta_flat = meta[...].reshape(n * META, LANES)
-    turned = meta_flat.T
+    for o in range(n):
+        for t, row in enumerate(look(meta[o][1:2, :], 2)):
+            square[3 * o + t : 3 * o + t + 1, :] = row
+    turned = square[...].T
     for o in range(n):
         for t in range(3):
-            lane = o * META + 1 + t
+            lane = 3 * o + t
             policy_terms[t, o * pol : (o + 1) * pol, :] = jnp.broadcast_to(
                 turned[0:pol, lane : lane + 1], (pol, LANES)
             )
-            lane = o * META + 5 + t
-            program_terms[o, t] = jnp.broadcast_to(turned[0:prog, lane : lane + 1], (prog, LANES))
-
-    policy_iota = lax.broadcasted_iota(jnp.int32, (n * pol, sites), 0).astype(f32)
+
+    policy_iota = lax.broadcasted_iota(jnp.int32, (n * pol, sites), 0)
     order = [0]
     for k in range(1, half + 1):
         order += [k] if k == groups - k else [k, groups - k]
@@ -247,21 +262,15 @@
         values = recv[pl.ds(2 * g, 2)].reshape(2 * sites, width)
         acc[...] += jnp.dot(pick, values, preferred_element_type=f32)
 
-    def policy_step(i, c):
-        d = lax.rem(me + n // 2 + i, n)
+    for k in route(n) + [0]:
+        d = across(me, k, n)
         at = pl.ds(pl.multiple_of(d * pol, pol), pol)
         spread = [
             jnp.concatenate([policy_terms[t, at, :]] * (width // LANES), axis=1) for t in range(3)
         ]
         losses[at, :] = terms(acc[at, :], *spread).astype(bf16)
-
-        @pl.when(d != me)
-        def _():
+        if k:
             policy_copy(d, me).start()
-
-        return c
-
-    lax.fori_loop(0, n, policy_step, 0)
     own_policy = pltpu.make_async_copy(
         losses.at[pl.ds(pl.multiple_of(me * pol, pol), pol), :],
         policy_out.at[:, pl.ds(pl.multiple_of(me * width, width), width)],
@@ -269,18 +278,16 @@
     )
     own_policy.start()
 
-    program_iota = lax.broadcasted_iota(jnp.int32, (n * prog, pol), 0).astype(f32)
+    program_iota = lax.broadcasted_iota(jnp.int32, (n * prog, pol), 0)
     marks = [
-        (program_iota == meta_flat[o * META + 4 : o * META + 5, 0:pol]).astype(bf16)
+        (program_iota == meta[o][1:2, pol : 2 * pol]).astype(bf16)
         for o in range(n)
     ]
     program_gross = jnp.dot(jnp.concatenate(marks, axis=1), losses[...], preferred_element_type=f32)
     for o in range(n):
-        spread = [
-            jnp.concatenate([program_terms[o, t]] * (width // LANES), axis=1) for t in range(3)
-        ]
-        program_send[o] = terms(program_gross[o * prog : (o + 1) * prog, :], *spread)
-    others(lambda d: program_copy(d, me).start())
+        program_send[o] = program_gross[o * prog : (o + 1) * prog, :]
+    for k in route(n):
+        program_copy(across(me, k, n), me).start()
     own_program = pltpu.make_async_copy(
         program_send.at[me],
         program_out.at[:, pl.ds(pl.multiple_of(me * width, width), width)],
@@ -299,6 +306,8 @@
     others(finish)
     own_policy.wait()
     own_program.wait()
+    spread = [jnp.concatenate([program_terms[t]] * (program_out.shape[1] // LANES), axis=1) for t in range(3)]
+    program_out[...] = terms(program_out[...], *spread)
 
 
 def exchange(
@@ -357,9 +366,9 @@
             pltpu.VMEM((3, items, LANES), f32),
             pltpu.VMEM((3, sites, LANES), f32),
             pltpu.VMEM((3, n * pol, LANES), f32),
-            pltpu.VMEM((n, 3, prog, LANES), f32),
+            pltpu.VMEM((3, prog, LANES), f32),
             pltpu.VMEM((sites, items), bf16),
-            pltpu.VMEM((n, META, LANES), f32),
+            pltpu.VMEM((n, 2, LANES), jnp.int32),
             pltpu.VMEM((n, sites, width), bf16),
             pltpu.VMEM((n, sites, width), bf16),
             pltpu.VMEM((n * pol, width), f32),
@@ -475,8 +484,8 @@
         sites, pol = rest[2].shape[0], rest[5].shape[0]
         prog = rest[6].shape[0]
         fits = cols % (n * LANES) == 0 and items % LANES == 0 and sites == LANES
-        fits = fits and pol <= LANES and pol % 16 == 0 and prog <= 8
-        fits = fits and n % 4 == 0 and n * META <= LANES and 3 * items <= LANES * (LANES - 3)
+        fits = fits and 2 * pol <= LANES and pol % 16 == 0 and prog <= 8
+        fits = fits and n % 4 == 0 and n & (n - 1) == 0 and 3 * n <= LANES and 3 * items <= LANES * (LANES - 6)
         return (exchange if fits else shards)(ground_up, item_site, item_profile, *rest)
 
     return jax.shard_map(

time: 33.3 us -> 33.1 us (level)
  no operation moved by 1% of the time
where the time goes in v3:
time: 33.1 us; the launch traced here: 32.9 us
  Pallas kernels  30.9 us (93%)
  local copies, waits for them, and re-layouts  1.31 us (4%)
  between operations  0.64 us (2%)
    pallas_call x1, Pallas kernels, exchange(): pl.pallas_call(functools.partial(kernel, n, pol, prog), out_shape=(pltpu....  30.9 us
    unnamed x2, local copies, waits for them, and re-layouts  1.31 us

profile of v3, /device:TPU:0, one launch (start us, length us, event | category | flops | bytes accessed | tf_op | source)
XLA Modules:
  0.0 32.9 jit_solution(15637849209375642343)
XLA Ops:
  0.6 30.9 %loss_terms.1 = (bf16[64,2048]{1,0:T(8,128)(2,1)S(1)}, f32[2,2048]{1,0:T(2,128)S(1)}) custom-call(bf16[512,2048]{1,0:T(8,128)(2,1)} %ground.1, s32[4,128]{1,0:T(4,128)} %bitcast.11, s32[4,128]{1,0:T(4,128)} %bitcast.12, s32[1,128]{1,0:T(1,128)} %bitcast.13, s32[1,128]{1,0:T(1,128)} %bitcast.14, s32[1,128]{1,0:T(1,128)} %bitcast.15, s32[1,64]{1,0:T(1,128)} %bitcast.16, ...), custom_call_target="tpu_custom_call" | custom-call | tf_op jit(solution)/shard_map/loss_terms/pallas_call | solution.py:353
  31.6 0.7 %copy.15 = bf16[64,2048]{1,0:T(8,128)(2,1)} copy(bf16[64,2048]{1,0:T(8,128)(2,1)S(1)} %get-tuple-element.2) | data formatting | bytes 524288
  32.3 0.6 %copy.16 = f32[2,2048]{1,0:T(2,128)} copy(f32[2,2048]{1,0:T(2,128)S(1)} %get-tuple-element.3) | data formatting | bytes 32768

commit v4 on v3

--- a/solution.py
+++ b/solution.py
@@ -54,6 +54,8 @@
         acc,
         losses,
         program_send,
+        marks,
+        picks,
         small_sem,
         load_sem,
         meta_ss,
@@ -242,13 +244,19 @@
             )
 
     policy_iota = lax.broadcasted_iota(jnp.int32, (n * pol, sites), 0)
-    order = [0]
-    for k in range(1, half + 1):
-        order += [k] if k == groups - k else [k, groups - k]
+    program_iota = lax.broadcasted_iota(jnp.int32, (n * prog, pol), 0)
+    marks[...] = jnp.concatenate(
+        [(program_iota == meta[o][1:2, pol : 2 * pol]).astype(bf16) for o in range(n)], axis=1
+    )
+    for k in range(groups):
+        g = across(mine, k, groups)
+        picks[k] = jnp.concatenate(
+            [(policy_iota == meta[2 * g + j][0:1, :]).astype(bf16) for j in range(2)], axis=1
+        )
     acc[...] = jnp.zeros_like(acc)
 
-    for k in order:
-        g = lax.rem(mine + k, groups)
+    for k in range(groups):
+        g = across(mine, k, groups)
         for j in range(2):
             s = 2 * g + j
 
@@ -256,11 +264,8 @@
             def _():
                 site_copy(me, s).wait_recv()
 
-        pick = jnp.concatenate(
-            [(policy_iota == meta[2 * g + j][0:1, :]).astype(bf16) for j in range(2)], axis=1
-        )
         values = recv[pl.ds(2 * g, 2)].reshape(2 * sites, width)
-        acc[...] += jnp.dot(pick, values, preferred_element_type=f32)
+        acc[...] += jnp.dot(picks[k], values, preferred_element_type=f32)
 
     for k in route(n) + [0]:
         d = across(me, k, n)
@@ -278,12 +283,7 @@
     )
     own_policy.start()
 
-    program_iota = lax.broadcasted_iota(jnp.int32, (n * prog, pol), 0)
-    marks = [
-        (program_iota == meta[o][1:2, pol : 2 * pol]).astype(bf16)
-        for o in range(n)
-    ]
-    program_gross = jnp.dot(jnp.concatenate(marks, axis=1), losses[...], preferred_element_type=f32)
+    program_gross = jnp.dot(marks[...], losses[...], preferred_element_type=f32)
     for o in range(n):
         program_send[o] = program_gross[o * prog : (o + 1) * prog, :]
     for k in route(n):
@@ -374,6 +374,8 @@
             pltpu.VMEM((n * pol, width), f32),
             pltpu.VMEM((n * pol, width), bf16),
             pltpu.VMEM((n, prog, width), f32),
+            pltpu.VMEM((n * prog, n * pol), bf16),
+            pltpu.VMEM((n // 2, n * pol, 2 * sites), bf16),
             dma((SMALL,)),
             dma((n // 2,)),
         ]

time: 33.1 us -> 32.7 us (0.988)
    pallas_call x1, Pallas kernels: 30.9 us -> 30.6 us  [exchange(): pl.pallas_call(functools.partial(kernel, n, pol, prog), out_shape=(pltpu....]
where the time goes in v4:
time: 32.7 us; the launch traced here: 32.5 us
  Pallas kernels  30.6 us (94%)
  local copies, waits for them, and re-layouts  1.31 us (4%)
  between operations  0.64 us (2%)
    pallas_call x1, Pallas kernels, exchange(): pl.pallas_call(functools.partial(kernel, n, pol, prog), out_shape=(pltpu....  30.6 us
    unnamed x2, local copies, waits for them, and re-layouts  1.31 us

profile of v4, /device:TPU:0, one launch (start us, length us, event | category | flops | bytes accessed | tf_op | source)
XLA Modules:
  0.0 32.5 jit_solution(2195553640953068756)
XLA Ops:
  0.6 30.6 %loss_terms.1 = (bf16[64,2048]{1,0:T(8,128)(2,1)S(1)}, f32[2,2048]{1,0:T(2,128)S(1)}) custom-call(bf16[512,2048]{1,0:T(8,128)(2,1)} %ground.1, s32[4,128]{1,0:T(4,128)} %bitcast.11, s32[4,128]{1,0:T(4,128)} %bitcast.12, s32[1,128]{1,0:T(1,128)} %bitcast.13, s32[1,128]{1,0:T(1,128)} %bitcast.14, s32[1,128]{1,0:T(1,128)} %bitcast.15, s32[1,64]{1,0:T(1,128)} %bitcast.16, ...), custom_call_target="tpu_custom_call" | custom-call | tf_op jit(solution)/shard_map/loss_terms/pallas_call | solution.py:353
  31.2 0.7 %copy.15 = bf16[64,2048]{1,0:T(8,128)(2,1)} copy(bf16[64,2048]{1,0:T(8,128)(2,1)S(1)} %get-tuple-element.2) | data formatting | bytes 524288
  31.9 0.6 %copy.16 = f32[2,2048]{1,0:T(2,128)} copy(f32[2,2048]{1,0:T(2,128)S(1)} %get-tuple-element.3) | data formatting | bytes 32768
